TPU v7x, 32 devices: a whole 2x2x4 slice. The times are simulated.
32 devices in a mesh: aux: 8 (over y, x, core), pair: 4 (over z).
Axes of the slice: x: 2, y: 2, z: 4, core: 2. Of those that a mesh axis runs over, the one named last changes fastest.
Arguments:
- integrals: bfloat16 [3072, 32768], P('aux', 'pair'), may hold values from -0.15625 to 0.15625
- densities: bfloat16 [16, 32768], P(None, 'pair'), may hold values from -2.390625 to 2.390625
- screen: int32 [24, 256], P('aux', 'pair'), may hold values 0 or 1
- factor: float32 [3072, 3072], P('aux', 'pair'), may hold values from -0.109375 to 0.109375
- diag_inv: float32 [3072, 768], P('aux'), may hold values from -2 to 2, as said below
Outputs:
- coulomb: float32 [16, 32768], P(None, ('pair', 'aux'))
Inputs may be any that keep to these rules, and one draw needn't show every extreme that they name: `diag_inv`: each block of 768 rows is an upper triangular matrix with a positive diagonal.
All inputs are finite; a program needn't handle non-finite values. No bound on the sum of `screen` on one device may be relied on, other than what follows from the above.
Results may differ from a plain program's by a relative error of at most 0.0041.
Values may be sent and summed in bfloat16 or wider, within the bound.
A program may use at most 128 MiB of HBM per device.

v0:
```python
import jax
import jax.numpy as jnp
from jax import lax
from jax.sharding import PartitionSpec as P

TILE = 128
SOLVE_BLOCKS = 4


def shards(integrals, densities, screen, factor, diag_inv):
    height = integrals.shape[0]
    breadth = factor.shape[1]
    block_size = diag_inv.shape[1]
    rows_aux = lax.axis_size("aux")
    total = height * rows_aux
    members = rows_aux // SOLVE_BLOCKS
    my_row = lax.axis_index("aux")
    my_column = lax.axis_index("pair")
    my_block = my_row // members
    count = densities.shape[0]
    highest = lax.Precision.HIGHEST
    expanded = jnp.repeat(jnp.repeat(screen, TILE, axis=0), TILE, axis=1).astype(jnp.bfloat16)
    masked = integrals * expanded
    partial_fit = lax.dot_general(
        densities, masked, (((1,), (1,)), ((), ())), preferred_element_type=jnp.float32
    )
    column_block = (my_column * breadth + jnp.arange(breadth, dtype=jnp.int32)) // block_size
    factor_low = jnp.where((column_block < my_block)[None, :], factor, 0.0)

    def apply_inverse(values):
        return jnp.dot(values, diag_inv, precision=highest, preferred_element_type=jnp.float32)

    def own_columns(whole):
        return lax.dynamic_slice_in_dim(whole, my_column * breadth, breadth, 1)

    def times_factor(known):
        return lax.dot_general(
            known,
            factor_low,
            (((1,), (1,)), ((), ())),
            precision=highest,
            preferred_element_type=jnp.float32,
        )

    zero_block = jnp.zeros((count, block_size), jnp.float32)
    solved = jnp.zeros((count, total), jnp.float32)
    for k in range(SOLVE_BLOCKS):

        def on_group(current):
            return apply_inverse(partial_fit - times_factor(own_columns(current)))

        def off_group(current):
            return zero_block

        summand = lax.cond(my_block == k, on_group, off_group, solved)
        arrived = lax.psum(summand, ("aux", "pair"))
        solved = lax.dynamic_update_slice_in_dim(solved, arrived, k * block_size, 1)
    own_coef = jnp.zeros((count, height), jnp.float32)
    contrib = jnp.zeros((count, total), jnp.float32)
    for target in reversed(range(SOLVE_BLOCKS)):
        if target < SOLVE_BLOCKS - 1:
            portion = contrib[:, target * block_size : (target + 1) * block_size]
            behind = lax.psum(portion, ("aux", "pair"))
            settled = solved[:, target * block_size : (target + 1) * block_size] - behind
        else:
            settled = solved[:, target * block_size : (target + 1) * block_size]

        def on_group(state):
            coef = lax.dot_general(
                settled,
                diag_inv,
                (((1,), (1,)), ((), ())),
                precision=highest,
                preferred_element_type=jnp.float32,
            )
            if target > 0:
                spread_out = jnp.dot(
                    coef, factor_low, precision=highest, preferred_element_type=jnp.float32
                )
                fresh = lax.dynamic_update_slice_in_dim(
                    jnp.zeros((count, total), jnp.float32), spread_out, my_column * breadth, 1
                )
            else:
                fresh = state[1]
            return (coef, fresh)

        def keep_state(state):
            return state

        own_coef, contrib = lax.cond(my_block == target, on_group, keep_state, (own_coef, contrib))
    rounded = own_coef.astype(jnp.bfloat16)
    summand = jnp.dot(rounded, masked, preferred_element_type=jnp.float32)
    result = lax.psum_scatter(summand, "aux", scatter_dimension=1, tiled=True)
    return result


def solution(mesh):
    in_specs = (
        P("aux", "pair"),
        P(None, "pair"),
        P("aux", "pair"),
        P("aux", "pair"),
        P("aux", None),
    )
    out_specs = P(None, ("pair", "aux"))
    return jax.shard_map(shards, mesh=mesh, in_specs=in_specs, out_specs=out_specs, check_vma=False)
```

profile of v0, /device:TPU:0, one launch (start us, length us, event | category | flops | bytes accessed | tf_op | source)
XLA Modules:
  0.0 370.9 jit_solution(1663735948647780986)
XLA Ops:
  6.5 0.0 copy-start
  6.5 0.0 reduce-scatter.2.cloned.1.call-start
  6.6 0.7 convert_element_type.40
  7.3 1.3 broadcast_select_fusion
  8.7 0.0 copy-start.3
  8.7 3.8 %broadcast_in_dim.25 = bf16[384,64,128]{2,1,0:T(8,128)(2,1)S(1)} broadcast(bf16[384,64]{1,0:T(8,128)(2,1)S(1)} %bitcast.36), dimensions={0,1} | broadcast | bytes 6340608 | tf_op jit(solution)/shard_map/broadcast_in_dim | solution.py:22
  12.5 0.0 copy-start.2
  12.5 0.0 copy-done
  12.5 0.0 copy-done.3
  12.5 0.0 copy-start.1
  12.6 4.0 %fusion.18 = f32[16,384]{1,0:T(8,128)S(1)} fusion(bf16[16,8192]{1,0:T(8,128)(2,1)S(1)} %copy-done, bf16[384,8192]{1,0:T(8,128)(2,1)S(1)} %copy-done.3, bf16[48,8,64,128]{3,2,1,0:T(8,128)(2,1)S(1)} %bitcast.34), kind=kOutput, calls=%fused_computation.26 | convolution fusion | flops 103809024 | bytes 12869632 | tf_op jit(solution)/shard_map/dot_general | solution.py:24
  16.5 0.0 copy-done.2
  16.5 0.0 copy-done.1
  16.5 1.8 conditional.8
  16.6 1.1 convolution_subtract_fusion
  17.6 0.7 fusion.22
  18.3 41.4 %psum.49 = f32[16,768]{1,0:T(8,128)S(1)} all-reduce(f32[16,768]{1,0:T(8,128)S(1)} %get-tuple-element.168), channel_id=1, replica_groups=mesh['aux'=8,'pair'=4] {'aux','pair'}, use_global_device_ids=true, to_apply=%region_2.3 | all-reduce | flops 12288 | bytes 98304 | tf_op jit(solution)/shard_map/psum | solution.py:56
  59.8 41.6 %psum.50 = f32[16,768]{1,0:T(8,128)S(1)} all-reduce(f32[16,768]{1,0:T(8,128)S(1)} %get-tuple-element.169), channel_id=1, replica_groups=mesh['aux'=8,'pair'=4] {'aux','pair'}, use_global_device_ids=true, to_apply=%region_5.6 | all-reduce | flops 12288 | bytes 98304 | tf_op jit(solution)/shard_map/psum | solution.py:56
  101.5 40.8 %psum.51 = f32[16,768]{1,0:T(8,128)S(1)} all-reduce(f32[16,768]{1,0:T(8,128)S(1)} %get-tuple-element.170), channel_id=1, replica_groups=mesh['aux'=8,'pair'=4] {'aux','pair'}, use_global_device_ids=true, to_apply=%region_8.9 | all-reduce | flops 12288 | bytes 98304 | tf_op jit(solution)/shard_map/psum | solution.py:56
  142.3 0.2 conditional.11
  142.5 43.4 %psum.52 = f32[16,768]{1,0:T(8,128)S(1)} all-reduce(f32[16,768]{1,0:T(8,128)S(1)} %get-tuple-element.171), channel_id=1, replica_groups=mesh['aux'=8,'pair'=4] {'aux','pair'}, use_global_device_ids=true, to_apply=%region_11.12 | all-reduce | flops 12288 | bytes 98304 | tf_op jit(solution)/shard_map/psum | solution.py:56
  185.9 1.3 conditional.12
  185.9 0.6 broadcast_in_dim.17
  186.5 0.7 broadcast.57
  187.2 0.8 slice.19
  188.0 42.1 %psum.53 = f32[16,768]{1,0:T(8,128)S(1)} all-reduce(f32[16,768]{1,0:T(8,128)S(1)} %slice.19), channel_id=1, replica_groups=mesh['aux'=8,'pair'=4] {'aux','pair'}, use_global_device_ids=true, to_apply=%region_14.15 | all-reduce | flops 12288 | bytes 98304 | tf_op jit(solution)/shard_map/psum | solution.py:63
  230.1 0.8 slice.20
  230.9 44.2 %psum.54 = f32[16,768]{1,0:T(8,128)S(1)} all-reduce(f32[16,768]{1,0:T(8,128)S(1)} %slice.20), channel_id=1, replica_groups=mesh['aux'=8,'pair'=4] {'aux','pair'}, use_global_device_ids=true, to_apply=%region_17.18 | all-reduce | flops 12288 | bytes 98304 | tf_op jit(solution)/shard_map/psum | solution.py:63
  275.1 0.8 slice.21
  276.0 43.3 %psum.55 = f32[16,768]{1,0:T(8,128)S(1)} all-reduce(f32[16,768]{1,0:T(8,128)S(1)} %slice.21), channel_id=1, replica_groups=mesh['aux'=8,'pair'=4] {'aux','pair'}, use_global_device_ids=true, to_apply=%region_20.21 | all-reduce | flops 12288 | bytes 98304 | tf_op jit(solution)/shard_map/psum | solution.py:63
  319.3 1.7 conditional.15
  319.3 1.7 fusion.13
  321.0 9.1 %fusion.16 = f32[16,8192]{1,0:T(8,128)} fusion(bf16[384,8192]{1,0:T(8,128)(2,1)} %param.21, bf16[48,8,64,128]{3,2,1,0:T(8,128)(2,1)} %bitcast.35, f32[16,384]{1,0:T(8,128)} %get-tuple-element.174), kind=kOutput, calls=%fused_computation.24 | convolution fusion | flops 103815168 | bytes 13131776 | tf_op jit(solution)/shard_map/dot_general | solution.py:92
  330.1 0.0 reduce-scatter.2.cloned.1.call-update
  330.1 33.9 %reduce-scatter.2.cloned.1.call-done = f32[16,1024]{1,0:T(8,128)} async-done(((f32[16,8192]{1,0:T(8,128)}), f32[16,1024]{1,0:T(8,128)}) %reduce-scatter.2.cloned.1.call-update) | async-done | bytes 65552 | tf_op jit(solution)/shard_map/reduce_scatter | solution.py:93
  (12 shorter events, 0.1 us)
Async XLA Ops:
  6.5 6.0 %copy-start = (bf16[16,8192]{1,0:T(8,128)(2,1)S(1)}, bf16[16,8192]{1,0:T(8,128)(2,1)}, u32[]{:S(2)}) copy-start(bf16[16,8192]{1,0:T(8,128)(2,1)} %param.22) | copy-start | bytes 786436
  6.5 357.5 %reduce-scatter.2.cloned.1.call-start = ((), (), s32[]{:S(2)}) async-start(), calls=%async_computation.1 | async-start | bytes 589824 | tf_op jit(solution)/shard_map/reduce_scatter | solution.py:93
  8.7 3.9 %copy-start.3 = (bf16[384,8192]{1,0:T(8,128)(2,1)S(1)}, bf16[384,8192]{1,0:T(8,128)(2,1)}, u32[]{:S(2)}) copy-start(bf16[384,8192]{1,0:T(8,128)(2,1)} %param.21) | copy-start | bytes 18874372
  12.5 4.0 %copy-start.2 = (bf16[384,64,128]{2,1,0:T(8,128)(2,1)}, bf16[384,64,128]{2,1,0:T(8,128)(2,1)S(1)}, u32[]{:S(2)}) copy-start(bf16[384,64,128]{2,1,0:T(8,128)(2,1)S(1)} %broadcast_in_dim.25) | copy-start | bytes 18874372
  12.5 4.0 %copy-start.1 = (f32[384,768]{1,0:T(8,128)S(1)}, f32[384,768]{1,0:T(8,128)}, u32[]{:S(2)}) copy-start(f32[384,768]{1,0:T(8,128)} %param.25) | copy-start | bytes 3538948
Sparse Core Ops, SparseCore 0:
  330.2 33.7 reduce-scatter.1
where the time goes:
time: 372 us; the launch traced here: 371 us
  blocking collectives  297 us (80%)
  waiting for transfers between devices  34 us (9%)
  matrix products  16.6 us (4%)
  between operations  13.6 us (4%)
  local copies, waits for them, and re-layouts  7.62 us (2%)
    psum x4, blocking collectives, shards(): arrived = lax.psum(summand, ('aux', 'pair'))  167 us
    psum x3, blocking collectives, shards(): behind = lax.psum(portion, ('aux', 'pair'))  130 us
    reduce_scatter x1, waiting for transfers between devices, shards(): result = lax.psum_scatter(summand, 'aux', scatter_dimension=1, tiled=True)  33.9 us
    dot_general x1, matrix products, shards(): summand = jnp.dot(rounded, masked, preferred_element_type=jnp.float32)  9.1 us
  transfers between devices with their start and end apart: 1, of which 1 were waited for; matrix products, arithmetic and copies ran while one was open for 0% of the time, Pallas kernels for 0%

commit v1 on v0

--- a/solution.py
+++ b/solution.py
@@ -60,7 +60,7 @@
     for target in reversed(range(SOLVE_BLOCKS)):
         if target < SOLVE_BLOCKS - 1:
             portion = contrib[:, target * block_size : (target + 1) * block_size]
-            behind = lax.psum(portion, ("aux", "pair"))
+            behind = jnp.sum(lax.all_gather(portion, ("aux", "pair")), axis=0)
             settled = solved[:, target * block_size : (target + 1) * block_size] - behind
         else:
             settled = solved[:, target * block_size : (target + 1) * block_size]

time: 372 us -> 421 us (1.13)
  waiting for transfers between devices: 34 us -> 210 us
  blocking collectives: 297 us -> 167 us
    all_gather x0 -> x3, waiting for transfers between devices: none -> 177 us  [shards(): behind = jnp.sum(lax.all_gather(portion, ('aux', 'pair')), axis=0)]
    psum x3 -> x0, blocking collectives: 130 us -> none  [shards(): behind = lax.psum(portion, ('aux', 'pair'))]
  transfers between devices with their start and end apart: 1 -> 4, of which waited for: 1 -> 4; matrix products, arithmetic and copies ran while one was open for 0% -> 0% of each run, Pallas kernels for 0% -> 0%
where the time goes in v1:
time: 421 us; the launch traced here: 420 us
  waiting for transfers between devices  210 us (50%)
  blocking collectives  167 us (40%)
  matrix products  16.6 us (4%)
  between operations  13.3 us (3%)
  local copies, waits for them, and re-layouts  9.47 us (2%)
    all_gather x3, waiting for transfers between devices, shards(): behind = jnp.sum(lax.all_gather(portion, ('aux', 'pair')), axis=0)  177 us
    psum x4, blocking collectives, shards(): arrived = lax.psum(summand, ('aux', 'pair'))  167 us
    reduce_scatter x1, waiting for transfers between devices, shards(): result = lax.psum_scatter(summand, 'aux', scatter_dimension=1, tiled=True)  32.3 us
    dot_general x1, matrix products, shards(): summand = jnp.dot(rounded, masked, preferred_element_type=jnp.float32)  9.12 us
  transfers between devices with their start and end apart: 4, of which 4 were waited for; matrix products, arithmetic and copies ran while one was open for 0% of the time, Pallas kernels for 0%

profile of v1, /device:TPU:0, one launch (start us, length us, event | category | flops | bytes accessed | tf_op | source)
XLA Modules:
  0.0 420.2 jit_solution(17415658657768113657)
XLA Ops:
  6.5 0.0 copy-start
  6.5 0.0 all-gather.7.cloned.1.call-start
  6.6 0.7 convert_element_type.40
  7.3 1.3 broadcast_select_fusion
  8.7 0.0 copy-start.3
  8.7 3.8 broadcast_in_dim.25
  12.5 0.0 copy-start.2
  12.5 0.0 copy-done
  12.5 0.0 copy-done.3
  12.5 0.0 copy-start.1
  12.6 4.0 fusion.18
  16.5 0.0 copy-done.2
  16.5 0.0 copy-done.1
  16.5 1.8 conditional.8
  16.6 1.1 convolution_subtract_fusion
  17.6 0.7 fusion.22
  18.3 41.4 %psum.28 = f32[16,768]{1,0:T(8,128)S(1)} all-reduce(f32[16,768]{1,0:T(8,128)S(1)} %get-tuple-element.174), channel_id=1, replica_groups=mesh['aux'=8,'pair'=4] {'aux','pair'}, use_global_device_ids=true, to_apply=%region_2.3 | all-reduce | flops 12288 | bytes 98304 | tf_op jit(solution)/shard_map/psum | solution.py:56
  59.8 41.6 %psum.29 = f32[16,768]{1,0:T(8,128)S(1)} all-reduce(f32[16,768]{1,0:T(8,128)S(1)} %get-tuple-element.175), channel_id=1, replica_groups=mesh['aux'=8,'pair'=4] {'aux','pair'}, use_global_device_ids=true, to_apply=%region_5.6 | all-reduce | flops 12288 | bytes 98304 | tf_op jit(solution)/shard_map/psum | solution.py:56
  101.5 40.8 %psum.30 = f32[16,768]{1,0:T(8,128)S(1)} all-reduce(f32[16,768]{1,0:T(8,128)S(1)} %get-tuple-element.176), channel_id=1, replica_groups=mesh['aux'=8,'pair'=4] {'aux','pair'}, use_global_device_ids=true, to_apply=%region_8.9 | all-reduce | flops 12288 | bytes 98304 | tf_op jit(solution)/shard_map/psum | solution.py:56
  142.3 0.2 conditional.11
  142.5 43.4 %psum.31 = f32[16,768]{1,0:T(8,128)S(1)} all-reduce(f32[16,768]{1,0:T(8,128)S(1)} %get-tuple-element.177), channel_id=1, replica_groups=mesh['aux'=8,'pair'=4] {'aux','pair'}, use_global_device_ids=true, to_apply=%region_11.12 | all-reduce | flops 12288 | bytes 98304 | tf_op jit(solution)/shard_map/psum | solution.py:56
  185.9 1.3 conditional.12
  186.0 0.6 broadcast_in_dim.17
  186.6 0.7 broadcast.57
  187.2 1.4 slice.19
  188.7 0.0 all-gather.7.cloned.1.call-update
  188.7 0.0 all-gather.9.cloned.1.call-start
  188.7 57.5 %all-gather.7.cloned.1.call-done = f32[512,768]{1,0:T(8,128)} async-done(((f32[16,768]{1,0:T(8,128)}), f32[512,768]{1,0:T(8,128)}) %all-gather.7.cloned.1.call-update) | async-done | bytes 1572880 | tf_op jit(solution)/shard_map/all_gather | solution.py:63
  246.2 1.4 slice.20
  247.7 0.0 all-gather.9.cloned.1.call-update
  247.7 0.0 all-gather.11.cloned.1.call-start
  247.7 59.9 %all-gather.9.cloned.1.call-done = f32[512,768]{1,0:T(8,128)} async-done(((f32[16,768]{1,0:T(8,128)}), f32[512,768]{1,0:T(8,128)}) %all-gather.9.cloned.1.call-update) | async-done | bytes 1572880 | tf_op jit(solution)/shard_map/all_gather | solution.py:63
  307.7 1.4 slice.21
  309.1 0.0 all-gather.11.cloned.1.call-update
  309.1 0.0 reduce-scatter.2.cloned.1.call-start
  309.2 59.9 %all-gather.11.cloned.1.call-done = f32[512,768]{1,0:T(8,128)} async-done(((f32[16,768]{1,0:T(8,128)}), f32[512,768]{1,0:T(8,128)}) %all-gather.11.cloned.1.call-update) | async-done | bytes 1572880 | tf_op jit(solution)/shard_map/all_gather | solution.py:63
  369.0 3.2 conditional.15
  369.0 1.5 reduce_sum.27
  370.5 1.7 fusion.13
  372.2 9.1 %fusion.16 = f32[16,8192]{1,0:T(8,128)} fusion(bf16[384,8192]{1,0:T(8,128)(2,1)} %param.21, bf16[48,8,64,128]{3,2,1,0:T(8,128)(2,1)} %bitcast.38, f32[16,384]{1,0:T(8,128)} %get-tuple-element.180), kind=kOutput, calls=%fused_computation.24 | convolution fusion | flops 103815168 | bytes 13131776 | tf_op jit(solution)/shard_map/dot_general | solution.py:92
  381.4 0.0 reduce-scatter.2.cloned.1.call-update
  381.4 32.3 %reduce-scatter.2.cloned.1.call-done = f32[16,1024]{1,0:T(8,128)} async-done(((f32[16,8192]{1,0:T(8,128)}), f32[16,1024]{1,0:T(8,128)}) %reduce-scatter.2.cloned.1.call-update) | async-done | bytes 65552 | tf_op jit(solution)/shard_map/reduce_scatter | solution.py:93
  (12 shorter events, 0.1 us)
Async XLA Ops:
  6.5 6.0 %copy-start = (bf16[16,8192]{1,0:T(8,128)(2,1)S(1)}, bf16[16,8192]{1,0:T(8,128)(2,1)}, u32[]{:S(2)}) copy-start(bf16[16,8192]{1,0:T(8,128)(2,1)} %param.22) | copy-start | bytes 786436
  6.5 239.7 %all-gather.7.cloned.1.call-start = ((), (), s32[]{:S(2)}) async-start(), calls=%async_computation.2 | async-start | bytes 1622016 | tf_op jit(solution)/shard_map/all_gather | solution.py:63
  8.7 3.9 copy-start.3
  12.5 4.0 copy-start.2
  12.5 4.0 copy-start.1
  188.7 119.0 %all-gather.9.cloned.1.call-start = ((), (), s32[]{:S(2)}) async-start(), calls=%async_computation.3 | async-start | bytes 1622016 | tf_op jit(solution)/shard_map/all_gather | solution.py:63
  247.7 121.3 %all-gather.11.cloned.1.call-start = ((), (), s32[]{:S(2)}) async-start(), calls=%async_computation.4 | async-start | bytes 1622016 | tf_op jit(solution)/shard_map/all_gather | solution.py:63
  309.1 104.6 %reduce-scatter.2.cloned.1.call-start = ((), (), s32[]{:S(2)}) async-start(), calls=%async_computation.1 | async-start | bytes 589824 | tf_op jit(solution)/shard_map/reduce_scatter | solution.py:93
Sparse Core Ops, SparseCore 0:
  188.8 57.3 all-gather.6
  249.1 58.4 all-gather.8
  310.5 58.4 all-gather.10
  381.5 32.1 reduce-scatter.1

commit v2 on v0

--- a/solution.py
+++ b/solution.py
@@ -53,7 +53,7 @@
             return zero_block
 
         summand = lax.cond(my_block == k, on_group, off_group, solved)
-        arrived = lax.psum(summand, ("aux", "pair"))
+        arrived = lax.psum(lax.psum(summand, "pair"), "aux")
         solved = lax.dynamic_update_slice_in_dim(solved, arrived, k * block_size, 1)
     own_coef = jnp.zeros((count, height), jnp.float32)
     contrib = jnp.zeros((count, total), jnp.float32)

time: 372 us -> 365 us (0.981)
  blocking collectives: 297 us -> 289 us
    psum x4 -> x8, blocking collectives: 167 us -> 162 us  [shards(): arrived = lax.psum(lax.psum(summand, 'pair'), 'aux')]
where the time goes in v2:
time: 365 us; the launch traced here: 364 us
  blocking collectives  289 us (79%)
  waiting for transfers between devices  34.2 us (9%)
  matrix products  16.6 us (5%)
  between operations  13.6 us (4%)
  local copies, waits for them, and re-layouts  7.62 us (2%)
    psum x8, blocking collectives, shards(): arrived = lax.psum(lax.psum(summand, 'pair'), 'aux')  162 us
    psum x3, blocking collectives, shards(): behind = lax.psum(portion, ('aux', 'pair'))  127 us
    reduce_scatter x1, waiting for transfers between devices, shards(): result = lax.psum_scatter(summand, 'aux', scatter_dimension=1, tiled=True)  34.1 us
    dot_general x1, matrix products, shards(): summand = jnp.dot(rounded, masked, preferred_element_type=jnp.float32)  9.11 us
  transfers between devices with their start and end apart: 1, of which 1 were waited for; matrix products, arithmetic and copies ran while one was open for 0% of the time, Pallas kernels for 0%

profile of v2, /device:TPU:0, one launch (start us, length us, event | category | flops | bytes accessed | tf_op | source)
XLA Modules:
  0.0 363.7 jit_solution(6197303659257777566)
XLA Ops:
  6.5 0.0 copy-start
  6.5 0.0 reduce-scatter.2.cloned.1.call-start
  6.6 0.7 convert_element_type.40
  7.3 1.3 broadcast_select_fusion
  8.7 0.0 copy-start.3
  8.7 3.8 %broadcast_in_dim.25 = bf16[384,64,128]{2,1,0:T(8,128)(2,1)S(1)} broadcast(bf16[384,64]{1,0:T(8,128)(2,1)S(1)} %bitcast.36), dimensions={0,1} | broadcast | bytes 6340608 | tf_op jit(solution)/shard_map/broadcast_in_dim | solution.py:22
  12.5 0.0 copy-start.2
  12.5 0.0 copy-done
  12.5 0.0 copy-done.3
  12.5 0.0 copy-start.1
  12.6 4.0 %fusion.18 = f32[16,384]{1,0:T(8,128)S(1)} fusion(bf16[16,8192]{1,0:T(8,128)(2,1)S(1)} %copy-done, bf16[384,8192]{1,0:T(8,128)(2,1)S(1)} %copy-done.3, bf16[48,8,64,128]{3,2,1,0:T(8,128)(2,1)S(1)} %bitcast.34), kind=kOutput, calls=%fused_computation.26 | convolution fusion | flops 103809024 | bytes 12869632 | tf_op jit(solution)/shard_map/dot_general | solution.py:24
  16.5 0.0 copy-done.2
  16.5 0.0 copy-done.1
  16.5 1.8 conditional.8
  16.6 1.1 convolution_subtract_fusion
  17.6 0.7 fusion.22
  18.3 21.3 %psum.77 = f32[16,768]{1,0:T(8,128)S(1)} all-reduce(f32[16,768]{1,0:T(8,128)S(1)} %get-tuple-element.168), channel_id=1, replica_groups=mesh['aux'=8,'pair'=4] {'pair'}, use_global_device_ids=true, to_apply=%region_2.3 | all-reduce | flops 12288 | bytes 98304 | tf_op jit(solution)/shard_map/psum | solution.py:56
  39.6 22.8 %psum.78 = f32[16,768]{1,0:T(8,128)S(1)} all-reduce(f32[16,768]{1,0:T(8,128)S(1)} %psum.77), channel_id=1, replica_groups=mesh['aux'=8,'pair'=4] {'aux'}, use_global_device_ids=true, to_apply=%region_3.4 | all-reduce | flops 12288 | bytes 98304 | tf_op jit(solution)/shard_map/psum | solution.py:56
  62.4 16.1 %psum.79 = f32[16,768]{1,0:T(8,128)S(1)} all-reduce(f32[16,768]{1,0:T(8,128)S(1)} %get-tuple-element.169), channel_id=1, replica_groups=mesh['aux'=8,'pair'=4] {'pair'}, use_global_device_ids=true, to_apply=%region_6.7 | all-reduce | flops 12288 | bytes 98304 | tf_op jit(solution)/shard_map/psum | solution.py:56
  78.6 22.8 %psum.80 = f32[16,768]{1,0:T(8,128)S(1)} all-reduce(f32[16,768]{1,0:T(8,128)S(1)} %psum.79), channel_id=1, replica_groups=mesh['aux'=8,'pair'=4] {'aux'}, use_global_device_ids=true, to_apply=%region_7.8 | all-reduce | flops 12288 | bytes 98304 | tf_op jit(solution)/shard_map/psum | solution.py:56
  101.4 17.9 %psum.81 = f32[16,768]{1,0:T(8,128)S(1)} all-reduce(f32[16,768]{1,0:T(8,128)S(1)} %get-tuple-element.170), channel_id=1, replica_groups=mesh['aux'=8,'pair'=4] {'pair'}, use_global_device_ids=true, to_apply=%region_10.11 | all-reduce | flops 12288 | bytes 98304 | tf_op jit(solution)/shard_map/psum | solution.py:56
  119.3 22.7 %psum.82 = f32[16,768]{1,0:T(8,128)S(1)} all-reduce(f32[16,768]{1,0:T(8,128)S(1)} %psum.81), channel_id=1, replica_groups=mesh['aux'=8,'pair'=4] {'aux'}, use_global_device_ids=true, to_apply=%region_11.12 | all-reduce | flops 12288 | bytes 98304 | tf_op jit(solution)/shard_map/psum | solution.py:56
  142.0 0.2 conditional.11
  142.3 16.1 %psum.83 = f32[16,768]{1,0:T(8,128)S(1)} all-reduce(f32[16,768]{1,0:T(8,128)S(1)} %get-tuple-element.171), channel_id=1, replica_groups=mesh['aux'=8,'pair'=4] {'pair'}, use_global_device_ids=true, to_apply=%region_14.15 | all-reduce | flops 12288 | bytes 98304 | tf_op jit(solution)/shard_map/psum | solution.py:56
  158.4 22.7 %psum.84 = f32[16,768]{1,0:T(8,128)S(1)} all-reduce(f32[16,768]{1,0:T(8,128)S(1)} %psum.83), channel_id=1, replica_groups=mesh['aux'=8,'pair'=4] {'aux'}, use_global_device_ids=true, to_apply=%region_15.16 | all-reduce | flops 12288 | bytes 98304 | tf_op jit(solution)/shard_map/psum | solution.py:56
  181.1 1.3 conditional.12
  181.1 0.6 broadcast_in_dim.17
  181.7 0.7 broadcast.57
  182.4 0.8 slice.19
  183.2 39.5 %psum.85 = f32[16,768]{1,0:T(8,128)S(1)} all-reduce(f32[16,768]{1,0:T(8,128)S(1)} %slice.19), channel_id=1, replica_groups=mesh['aux'=8,'pair'=4] {'aux','pair'}, use_global_device_ids=true, to_apply=%region_18.19 | all-reduce | flops 12288 | bytes 98304 | tf_op jit(solution)/shard_map/psum | solution.py:63
  222.8 0.8 slice.20
  223.6 44.8 %psum.86 = f32[16,768]{1,0:T(8,128)S(1)} all-reduce(f32[16,768]{1,0:T(8,128)S(1)} %slice.20), channel_id=1, replica_groups=mesh['aux'=8,'pair'=4] {'aux','pair'}, use_global_device_ids=true, to_apply=%region_21.22 | all-reduce | flops 12288 | bytes 98304 | tf_op jit(solution)/shard_map/psum | solution.py:63
  268.4 0.8 slice.21
  269.2 42.7 %psum.87 = f32[16,768]{1,0:T(8,128)S(1)} all-reduce(f32[16,768]{1,0:T(8,128)S(1)} %slice.21), channel_id=1, replica_groups=mesh['aux'=8,'pair'=4] {'aux','pair'}, use_global_device_ids=true, to_apply=%region_24.25 | all-reduce | flops 12288 | bytes 98304 | tf_op jit(solution)/shard_map/psum | solution.py:63
  311.9 1.7 conditional.15
  311.9 1.7 fusion.13
  313.6 9.1 %fusion.16 = f32[16,8192]{1,0:T(8,128)} fusion(bf16[384,8192]{1,0:T(8,128)(2,1)} %param.21, bf16[48,8,64,128]{3,2,1,0:T(8,128)(2,1)} %bitcast.35, f32[16,384]{1,0:T(8,128)} %get-tuple-element.174), kind=kOutput, calls=%fused_computation.24 | convolution fusion | flops 103815168 | bytes 13131776 | tf_op jit(solution)/shard_map/dot_general | solution.py:92
  322.7 0.0 reduce-scatter.2.cloned.1.call-update
  322.7 34.1 %reduce-scatter.2.cloned.1.call-done = f32[16,1024]{1,0:T(8,128)} async-done(((f32[16,8192]{1,0:T(8,128)}), f32[16,1024]{1,0:T(8,128)}) %reduce-scatter.2.cloned.1.call-update) | async-done | bytes 65552 | tf_op jit(solution)/shard_map/reduce_scatter | solution.py:93
  (12 shorter events, 0.1 us)
Async XLA Ops:
  6.5 6.0 %copy-start = (bf16[16,8192]{1,0:T(8,128)(2,1)S(1)}, bf16[16,8192]{1,0:T(8,128)(2,1)}, u32[]{:S(2)}) copy-start(bf16[16,8192]{1,0:T(8,128)(2,1)} %param.22) | copy-start | bytes 786436
  6.5 350.4 %reduce-scatter.2.cloned.1.call-start = ((), (), s32[]{:S(2)}) async-start(), calls=%async_computation.1 | async-start | bytes 589824 | tf_op jit(solution)/shard_map/reduce_scatter | solution.py:93
  8.7 3.9 %copy-start.3 = (bf16[384,8192]{1,0:T(8,128)(2,1)S(1)}, bf16[384,8192]{1,0:T(8,128)(2,1)}, u32[]{:S(2)}) copy-start(bf16[384,8192]{1,0:T(8,128)(2,1)} %param.21) | copy-start | bytes 18874372
  12.5 4.0 %copy-start.2 = (bf16[384,64,128]{2,1,0:T(8,128)(2,1)}, bf16[384,64,128]{2,1,0:T(8,128)(2,1)S(1)}, u32[]{:S(2)}) copy-start(bf16[384,64,128]{2,1,0:T(8,128)(2,1)S(1)} %broadcast_in_dim.25) | copy-start | bytes 18874372
  12.5 4.0 %copy-start.1 = (f32[384,768]{1,0:T(8,128)S(1)}, f32[384,768]{1,0:T(8,128)}, u32[]{:S(2)}) copy-start(f32[384,768]{1,0:T(8,128)} %param.25) | copy-start | bytes 3538948
Sparse Core Ops, SparseCore 0:
  322.9 33.9 reduce-scatter.1
